TPU v7x, 32 devices: a whole 2x2x4 slice. The times are simulated.
32 devices in a mesh: seq: 8 (over z, y), grp: 4 (over x, core).
Axes of the slice: x: 2, y: 2, z: 4, core: 2. Of those that a mesh axis runs over, the one named last changes fastest.
Arguments:
- hidden: bfloat16 [4096, 2048], P('seq', 'grp'), may hold values from -8 to 8
- qkv_weight: bfloat16 [3, 2048, 6144], P(None, 'seq', 'grp'), may hold values from -0.125 to 0.125
- out_weight: bfloat16 [3, 2048, 2048], P(None, 'grp', 'seq'), may hold values from -0.125 to 0.125
- projection: float32 [3, 16, 128, 128], P(None, 'grp'), may hold values from -6 to 6
- norm_gain: float32 [3, 2048], replicated, may hold values from 0.1 to 1.9
- out_gain: float32 [3, 2048], P(None, 'grp'), may hold values from 0.1 to 1.9
Outputs:
- layer_out: bfloat16 [4096, 2048], P('seq', 'grp')
All inputs are finite; a program needn't handle non-finite values.
Results may differ from a plain program's by a relative error of at most 0.034.
Values may be sent and summed in bfloat16 or wider, within the bound.
A program may use at most 64 MiB of HBM per device.

v0:
```python
import math
import jax
import jax.numpy as jnp
from jax import lax
from jax.sharding import PartitionSpec as P

stabilizer = 2.0
highest = lax.Precision.HIGHEST


def prefix(array, axis, combine, identity):
    peers, index = (lax.axis_size(axis), lax.axis_index(axis))
    everything = jax.tree.map(
        lambda part, kind: lax.all_gather(part.astype(kind), axis),
        array,
        (jnp.bfloat16, jnp.bfloat16),
    )
    start = jax.tree.map(
        lambda part, zero: jnp.broadcast_to(jnp.asarray(zero, part.dtype), part.shape),
        array,
        identity,
    )

    def step(k, before):
        reached = k < index
        new = combine(
            before, jax.tree.map(lambda part, own: part[k].astype(own.dtype), everything, array)
        )
        return jax.tree.map(lambda a, b: jnp.where(reached, a, b), new, before)

    return lax.fori_loop(0, peers, step, start)


def features(rows, projection_layer):
    head_size = rows.shape[-1]
    feature_count = projection_layer.shape[-1]
    scaled = rows.astype(jnp.float32) * head_size ** (-0.25)
    mixed = jnp.einsum("thd,hdm->thm", scaled, projection_layer, precision=highest)
    energy = 0.5 * jnp.sum(scaled * scaled, axis=-1, keepdims=True)
    return (jnp.exp(mixed - energy - stabilizer) / math.sqrt(feature_count)).astype(jnp.bfloat16)


def add_states(earlier, later):
    return (earlier[0] + later[0], earlier[1] + later[1])


def local(hidden, qkv_weight, out_weight, projection, norm_gain, out_gain):
    layer_count = qkv_weight.shape[0]
    local_heads = projection.shape[1]
    head_size = projection.shape[2]
    feature_count = projection.shape[3]
    token_rows = hidden.shape[0]
    stream = hidden
    causal_mask = jnp.arange(token_rows)[:, None] >= jnp.arange(token_rows)[None, :]
    for layer_index in range(layer_count):
        gathered = lax.all_gather(stream, "grp", axis=1, tiled=True)
        wide = gathered.astype(jnp.float32)
        inverse_rms = lax.rsqrt(jnp.mean(wide * wide, axis=-1, keepdims=True) + 1e-05)
        normed = (wide * inverse_rms * norm_gain[layer_index][None, :]).astype(jnp.bfloat16)
        qkv_wide = jnp.dot(
            normed,
            lax.all_gather(qkv_weight[layer_index], "seq", axis=0, tiled=True),
            preferred_element_type=jnp.float32,
        )
        qkv = qkv_wide.astype(jnp.bfloat16).reshape(token_rows, local_heads, 3, head_size)
        query_feat = features(qkv[:, :, 0], projection[layer_index])
        key_feat = features(qkv[:, :, 1], projection[layer_index])
        value_rows = qkv[:, :, 2]
        block_kv = jnp.einsum(
            "jhm,jhe->hme", key_feat, value_rows, preferred_element_type=jnp.float32
        )
        block_z = jnp.sum(key_feat.astype(jnp.float32), axis=0)
        zero_kv = jnp.zeros((local_heads, feature_count, head_size), jnp.float32)
        zero_z = jnp.zeros((local_heads, feature_count), jnp.float32)
        prefix_kv, prefix_z = prefix((block_kv, block_z), "seq", add_states, (zero_kv, zero_z))
        scores = jnp.einsum(
            "ihm,jhm->hij", query_feat, key_feat, preferred_element_type=jnp.float32
        )
        masked = jnp.where(causal_mask[None], scores, jnp.zeros_like(scores))
        score_weights = masked.astype(jnp.bfloat16)
        query_wide = query_feat.astype(jnp.float32)
        denominator = jnp.sum(masked, axis=-1) + jnp.einsum(
            "ihm,hm->hi", query_wide, prefix_z, precision=highest
        )
        numerator = jnp.einsum(
            "hij,jhe->hie", score_weights, value_rows, preferred_element_type=jnp.float32
        )
        numerator = numerator + jnp.einsum(
            "ihm,hme->hie",
            query_feat,
            prefix_kv.astype(jnp.bfloat16),
            preferred_element_type=jnp.float32,
        )
        attention = numerator / denominator[..., None]
        inverse_norm = lax.rsqrt(jnp.mean(attention * attention, axis=-1, keepdims=True) + 1e-06)
        head_gain = out_gain[layer_index].reshape(local_heads, head_size)[:, None, :]
        attended = (attention * inverse_norm * head_gain).astype(jnp.bfloat16)
        attended = jnp.transpose(attended, (1, 0, 2)).reshape(token_rows, local_heads * head_size)
        terms = jnp.dot(
            attended,
            lax.all_gather(out_weight[layer_index], "seq", axis=1, tiled=True),
            preferred_element_type=jnp.float32,
        )
        summed = lax.psum_scatter(
            terms.astype(jnp.bfloat16), "grp", scatter_dimension=1, tiled=True
        ).astype(jnp.float32)
        stream = (stream.astype(jnp.float32) + summed).astype(jnp.bfloat16)
    return stream


def solution(mesh):
    return jax.shard_map(
        local,
        mesh=mesh,
        in_specs=(
            P("seq", "grp"),
            P(None, "seq", "grp"),
            P(None, "grp", "seq"),
            P(None, "grp", None, None),
            P(),
            P(None, "grp"),
        ),
        out_specs=P("seq", "grp"),
        check_vma=False,
    )
```

profile of v0, /device:TPU:0, one launch (start us, length us, event | category | flops | bytes accessed | tf_op | source)
XLA Modules:
  0.0 804.3 jit_solution(3640511315558074532)
XLA Ops:
  7.3 3.1 fusion.132
  10.6 23.6 %all-gather.28.cloned.1.call-done = bf16[512,2048]{1,0:T(8,128)(2,1)} async-done(((bf16[512,512]{1,0:T(8,128)(2,1)}), bf16[512,2048]{1,0:T(8,128)(2,1)}) %all-gather.28.cloned.1.call-update) | async-done | bytes 2097168 | tf_op jit(solution)/shard_map/all_gather | solution.py:56
  34.2 2.2 fusion.6
  36.4 98.7 %all-gather.34.cloned.1.call-done = bf16[1,2048,1536]{2,1,0:T(8,128)(2,1)} async-done(((bf16[1,256,1536]{2,1,0:T(8,128)(2,1)}), bf16[1,2048,1536]{2,1,0:T(8,128)(2,1)}) %all-gather.34.cloned.1.call-update) | async-done | bytes 6291472 | tf_op jit(solution)/shard_map/all_gather | solution.py:62
  135.1 7.4 fusion.15
  142.6 1.7 copy.46
  145.0 2.3 fusion.139
  148.3 2.0 fusion.136
  151.3 17.7 %all-gather.12 = bf16[8,4,128]{2,1,0:T(4,128)(2,1)S(1)} all-gather(bf16[1,4,128]{2,1,0:T(4,128)(2,1)S(1)} %bitcast.327), channel_id=4, replica_groups=mesh['seq'=8,'grp'=4] {'seq'}, dimensions={0}, use_global_device_ids=true | all-gather | bytes 9216 | tf_op jit(solution)/shard_map/all_gather | solution.py:14
  169.6 2.2 fusion.77
  171.9 2.1 select_reduce_fusion.2
  174.0 13.0 %all-gather.36.cloned.1.call-done = bf16[32,128,128]{2,1,0:T(8,128)(2,1)} async-done(((bf16[4,128,128]{2,1,0:T(8,128)(2,1)}), bf16[32,128,128]{2,1,0:T(8,128)(2,1)}) %all-gather.36.cloned.1.call-update) | async-done | bytes 1048592 | tf_op jit(solution)/shard_map/all_gather | solution.py:14
  186.9 8.7 %while.48 = (s32[]{:T(128)}, f32[4,128,128]{2,1,0:T(8,128)S(1)}, f32[4,128]{1,0:T(4,128)S(1)}, s32[]{:T(128)}, bf16[8,4,128,128]{3,2,1,0:T(8,128)(2,1)}, /*index...) while((s32[]{:T(128)}, f32[4,128,128]{2,1,0:T(8,128)S(1)}, f32[4,128]{1,0:T(4,128)S(1)}, ...), condition=%wide.region_5.6_spmd.clone, body=%wide.region_4.5_spmd.clone.sunk | while | flops 264196 | bytes 660595 | solution.py:31
  186.9 1.1 add_select_fusion.12
  198.1 39.8 %all-gather.38.cloned.1.call-done = bf16[1,512,2048]{2,1,0:T(8,128)(2,1)} async-done(((bf16[1,512,256]{2,1,0:T(8,128)(2,1)}), bf16[1,512,2048]{2,1,0:T(8,128)(2,1)}) %all-gather.38.cloned.1.call-update) | async-done | bytes 2097168 | tf_op jit(solution)/shard_map/all_gather | solution.py:101
  237.9 4.2 convolution_convert_fusion.2
  242.2 29.4 %reduce-scatter.4.cloned.1.call-done = bf16[512,512]{1,0:T(8,128)(2,1)} async-done(((bf16[512,2048]{1,0:T(8,128)(2,1)}), bf16[512,512]{1,0:T(8,128)(2,1)}) %reduce-scatter.4.cloned.1.call-update) | async-done | bytes 524304 | tf_op jit(solution)/shard_map/reduce_scatter | solution.py:104
  271.6 2.0 add_convert_fusion.2
  274.6 21.8 %all-gather.30.cloned.1.call-done = bf16[512,2048]{1,0:T(8,128)(2,1)} async-done(((bf16[512,512]{1,0:T(8,128)(2,1)}), bf16[512,2048]{1,0:T(8,128)(2,1)}) %all-gather.30.cloned.1.call-update) | async-done | bytes 2097168 | tf_op jit(solution)/shard_map/all_gather | solution.py:56
  296.3 2.2 fusion.9
  298.6 98.7 %all-gather.40.cloned.1.call-done = bf16[1,2048,1536]{2,1,0:T(8,128)(2,1)} async-done(((bf16[1,256,1536]{2,1,0:T(8,128)(2,1)}), bf16[1,2048,1536]{2,1,0:T(8,128)(2,1)}) %all-gather.40.cloned.1.call-update) | async-done | bytes 6291472 | tf_op jit(solution)/shard_map/all_gather | solution.py:62
  397.3 7.4 fusion.18
  404.7 1.7 copy.54
  407.1 2.2 fusion.140
  411.2 17.7 %all-gather.13 = bf16[8,4,128]{2,1,0:T(4,128)(2,1)S(1)} all-gather(bf16[1,4,128]{2,1,0:T(4,128)(2,1)S(1)} %bitcast.329), channel_id=8, replica_groups=mesh['seq'=8,'grp'=4] {'seq'}, dimensions={0}, use_global_device_ids=true | all-gather | bytes 9216 | tf_op jit(solution)/shard_map/all_gather | solution.py:14
  429.6 2.2 fusion.75
  431.8 2.1 select_reduce_fusion.1
  433.9 15.0 %all-gather.42.cloned.1.call-done = bf16[32,128,128]{2,1,0:T(8,128)(2,1)} async-done(((bf16[4,128,128]{2,1,0:T(8,128)(2,1)}), bf16[32,128,128]{2,1,0:T(8,128)(2,1)}) %all-gather.42.cloned.1.call-update) | async-done | bytes 1048592 | tf_op jit(solution)/shard_map/all_gather | solution.py:14
  449.0 8.7 %while.49 = (s32[]{:T(128)}, f32[4,128,128]{2,1,0:T(8,128)S(1)}, f32[4,128]{1,0:T(4,128)S(1)}, s32[]{:T(128)}, bf16[8,4,128,128]{3,2,1,0:T(8,128)(2,1)}, /*index...) while((s32[]{:T(128)}, f32[4,128,128]{2,1,0:T(8,128)S(1)}, f32[4,128]{1,0:T(4,128)S(1)}, ...), condition=%wide.region_14.15_spmd.clone, body=%wide.region_13.14_spmd.clone.sunk | while | flops 264196 | bytes 660595 | solution.py:31
  460.1 40.0 %all-gather.44.cloned.1.call-done = bf16[1,512,2048]{2,1,0:T(8,128)(2,1)} async-done(((bf16[1,512,256]{2,1,0:T(8,128)(2,1)}), bf16[1,512,2048]{2,1,0:T(8,128)(2,1)}) %all-gather.44.cloned.1.call-update) | async-done | bytes 2097168 | tf_op jit(solution)/shard_map/all_gather | solution.py:101
  500.1 4.2 convolution_convert_fusion.1
  504.4 29.4 %reduce-scatter.6.cloned.1.call-done = bf16[512,512]{1,0:T(8,128)(2,1)} async-done(((bf16[512,2048]{1,0:T(8,128)(2,1)}), bf16[512,512]{1,0:T(8,128)(2,1)}) %reduce-scatter.6.cloned.1.call-update) | async-done | bytes 524304 | tf_op jit(solution)/shard_map/reduce_scatter | solution.py:104
  533.8 2.0 add_convert_fusion.1
  536.7 21.9 %all-gather.32.cloned.1.call-done = bf16[512,2048]{1,0:T(8,128)(2,1)} async-done(((bf16[512,512]{1,0:T(8,128)(2,1)}), bf16[512,2048]{1,0:T(8,128)(2,1)}) %all-gather.32.cloned.1.call-update) | async-done | bytes 2097168 | tf_op jit(solution)/shard_map/all_gather | solution.py:56
  558.6 2.2 fusion.12
  560.8 98.5 %all-gather.46.cloned.1.call-done = bf16[1,2048,1536]{2,1,0:T(8,128)(2,1)} async-done(((bf16[1,256,1536]{2,1,0:T(8,128)(2,1)}), bf16[1,2048,1536]{2,1,0:T(8,128)(2,1)}) %all-gather.46.cloned.1.call-update) | async-done | bytes 6291472 | tf_op jit(solution)/shard_map/all_gather | solution.py:62
  659.3 7.4 fusion.21
  666.7 1.7 copy.62
  669.2 2.3 fusion.141
  673.1 17.7 %all-gather.14 = bf16[8,4,128]{2,1,0:T(4,128)(2,1)S(1)} all-gather(bf16[1,4,128]{2,1,0:T(4,128)(2,1)S(1)} %bitcast.328), channel_id=12, replica_groups=mesh['seq'=8,'grp'=4] {'seq'}, dimensions={0}, use_global_device_ids=true | all-gather | bytes 9216 | tf_op jit(solution)/shard_map/all_gather | solution.py:14
  691.5 2.2 fusion.73
  693.7 2.1 select_reduce_fusion
  695.8 15.3 %all-gather.48.cloned.1.call-done = bf16[32,128,128]{2,1,0:T(8,128)(2,1)} async-done(((bf16[4,128,128]{2,1,0:T(8,128)(2,1)}), bf16[32,128,128]{2,1,0:T(8,128)(2,1)}) %all-gather.48.cloned.1.call-update) | async-done | bytes 1048592 | tf_op jit(solution)/shard_map/all_gather | solution.py:14
  711.1 8.7 %while.50 = (s32[]{:T(128)}, f32[4,128,128]{2,1,0:T(8,128)S(1)}, f32[4,128]{1,0:T(4,128)S(1)}, s32[]{:T(128)}, bf16[8,4,128,128]{3,2,1,0:T(8,128)(2,1)}, /*index...) while((s32[]{:T(128)}, f32[4,128,128]{2,1,0:T(8,128)S(1)}, f32[4,128]{1,0:T(4,128)S(1)}, ...), condition=%wide.region_23.24_spmd.clone, body=%wide.region_22.23_spmd.clone.sunk | while | flops 264196 | bytes 660595 | solution.py:31
  722.3 39.8 %all-gather.50.cloned.1.call-done = bf16[1,512,2048]{2,1,0:T(8,128)(2,1)} async-done(((bf16[1,512,256]{2,1,0:T(8,128)(2,1)}), bf16[1,512,2048]{2,1,0:T(8,128)(2,1)}) %all-gather.50.cloned.1.call-update) | async-done | bytes 2097168 | tf_op jit(solution)/shard_map/all_gather | solution.py:101
  762.1 4.2 convolution_convert_fusion
  766.3 29.5 %reduce-scatter.8.cloned.1.call-done = bf16[512,512]{1,0:T(8,128)(2,1)} async-done(((bf16[512,2048]{1,0:T(8,128)(2,1)}), bf16[512,512]{1,0:T(8,128)(2,1)}) %reduce-scatter.8.cloned.1.call-update) | async-done | bytes 524304 | tf_op jit(solution)/shard_map/reduce_scatter | solution.py:104
  795.8 2.0 add_convert_fusion
  (165 shorter events, 43.9 us)
Async XLA Ops:
  6.5 27.7 %all-gather.28.cloned.1.call-start = ((), (), s32[]{:S(2)}) async-start(), calls=%async_computation.3 | async-start | bytes 2621440 | tf_op jit(solution)/shard_map/all_gather | solution.py:56
  7.3 3.3 copy-start.12
  7.3 127.9 %all-gather.34.cloned.1.call-start = ((), (), s32[]{:S(2)}) async-start(), calls=%async_computation.9 | async-start | bytes 7077888 | tf_op jit(solution)/shard_map/all_gather | solution.py:62
  10.5 176.4 %all-gather.36.cloned.1.call-start = ((), (), s32[]{:S(2)}) async-start(), calls=%async_computation.10 | async-start | bytes 1179648 | tf_op jit(solution)/shard_map/all_gather | solution.py:14
  34.2 100.9 %copy-start.3 = (bf16[512,2048]{1,0:T(8,128)(2,1)S(1)}, bf16[512,2048]{1,0:T(8,128)(2,1)}, u32[]{:S(2)}) copy-start(bf16[512,2048]{1,0:T(8,128)(2,1)} %all-gather.28.cloned.1.call-done) | copy-start | bytes 6291460
  147.3 4.0 copy-start.13
  148.3 89.6 %all-gather.38.cloned.1.call-start = ((), (), s32[]{:S(2)}) async-start(), calls=%async_computation.11 | async-start | bytes 2359296 | tf_op jit(solution)/shard_map/all_gather | solution.py:101
  150.4 121.2 %reduce-scatter.4.cloned.1.call-start = ((), (), s32[]{:S(2)}) async-start(), calls=%async_computation.4 | async-start | bytes 2621440 | tf_op jit(solution)/shard_map/reduce_scatter | solution.py:104
  169.3 2.6 copy-start.6
  186.9 9.6 %copy-start.7 = (pred[512,512]{0,1:T(8,128)(4,1)S(1)}, pred[512,512]{0,1:T(8,128)(4,1)}, u32[]{:S(2)}) copy-start(pred[512,512]{0,1:T(8,128)(4,1)} %iota_compare_fusion) | copy-start | bytes 786436
  195.6 1.7 copy-start.15
  242.1 29.5 %copy-start.2 = (bf16[512,512]{1,0:T(8,128)(2,1)S(1)}, bf16[512,512]{1,0:T(8,128)(2,1)}, u32[]{:S(2)}) copy-start(bf16[512,512]{1,0:T(8,128)(2,1)} %param.12) | copy-start | bytes 1572868
  242.1 54.2 %all-gather.30.cloned.1.call-start = ((), (), s32[]{:S(2)}) async-start(), calls=%async_computation.5 | async-start | bytes 2621440 | tf_op jit(solution)/shard_map/all_gather | solution.py:56
  273.6 123.6 %all-gather.40.cloned.1.call-start = ((), (), s32[]{:S(2)}) async-start(), calls=%async_computation.12 | async-start | bytes 7077888 | tf_op jit(solution)/shard_map/all_gather | solution.py:62
  274.4 174.6 %all-gather.42.cloned.1.call-start = ((), (), s32[]{:S(2)}) async-start(), calls=%async_computation.13 | async-start | bytes 1179648 | tf_op jit(solution)/shard_map/all_gather | solution.py:14
  296.3 100.9 %copy-start.5 = (bf16[512,2048]{1,0:T(8,128)(2,1)S(1)}, bf16[512,2048]{1,0:T(8,128)(2,1)}, u32[]{:S(2)}) copy-start(bf16[512,2048]{1,0:T(8,128)(2,1)} %all-gather.30.cloned.1.call-done) | copy-start | bytes 6291460
  410.4 89.7 %all-gather.44.cloned.1.call-start = ((), (), s32[]{:S(2)}) async-start(), calls=%async_computation.14 | async-start | bytes 2359296 | tf_op jit(solution)/shard_map/all_gather | solution.py:101
  411.2 122.7 %reduce-scatter.6.cloned.1.call-start = ((), (), s32[]{:S(2)}) async-start(), calls=%async_computation.6 | async-start | bytes 2621440 | tf_op jit(solution)/shard_map/reduce_scatter | solution.py:104
  429.2 2.6 copy-start.8
  449.0 9.6 %copy-start.9 = (pred[512,512]{0,1:T(8,128)(4,1)S(1)}, pred[512,512]{0,1:T(8,128)(4,1)}, u32[]{:S(2)}) copy-start(pred[512,512]{0,1:T(8,128)(4,1)} %iota_compare_fusion) | copy-start | bytes 786436
  457.7 1.7 copy-start.16
  504.3 29.5 %copy-start.1 = (bf16[512,512]{1,0:T(8,128)(2,1)S(1)}, bf16[512,512]{1,0:T(8,128)(2,1)}, u32[]{:S(2)}) copy-start(bf16[512,512]{1,0:T(8,128)(2,1)} %add_convert_fusion.2) | copy-start | bytes 1572868
  504.3 54.2 %all-gather.32.cloned.1.call-start = ((), (), s32[]{:S(2)}) async-start(), calls=%async_computation.7 | async-start | bytes 2621440 | tf_op jit(solution)/shard_map/all_gather | solution.py:56
  535.8 123.5 %all-gather.46.cloned.1.call-start = ((), (), s32[]{:S(2)}) async-start(), calls=%async_computation.15 | async-start | bytes 7077888 | tf_op jit(solution)/shard_map/all_gather | solution.py:62
  536.4 174.7 %all-gather.48.cloned.1.call-start = ((), (), s32[]{:S(2)}) async-start(), calls=%async_computation.16 | async-start | bytes 1179648 | tf_op jit(solution)/shard_map/all_gather | solution.py:14
  558.5 100.8 %copy-start.4 = (bf16[512,2048]{1,0:T(8,128)(2,1)S(1)}, bf16[512,2048]{1,0:T(8,128)(2,1)}, u32[]{:S(2)}) copy-start(bf16[512,2048]{1,0:T(8,128)(2,1)} %all-gather.32.cloned.1.call-done) | copy-start | bytes 6291460
  672.5 89.6 %all-gather.50.cloned.1.call-start = ((), (), s32[]{:S(2)}) async-start(), calls=%async_computation.17 | async-start | bytes 2359296 | tf_op jit(solution)/shard_map/all_gather | solution.py:101
  673.1 122.7 %reduce-scatter.8.cloned.1.call-start = ((), (), s32[]{:S(2)}) async-start(), calls=%async_computation.8 | async-start | bytes 2621440 | tf_op jit(solution)/shard_map/reduce_scatter | solution.py:104
  691.1 2.6 copy-start.10
  711.1 9.6 %copy-start.11 = (pred[512,512]{0,1:T(8,128)(4,1)S(1)}, pred[512,512]{0,1:T(8,128)(4,1)}, u32[]{:S(2)}) copy-start(pred[512,512]{0,1:T(8,128)(4,1)} %iota_compare_fusion) | copy-start | bytes 786436
  719.8 1.7 copy-start.14
  766.3 29.5 %copy-start = (bf16[512,512]{1,0:T(8,128)(2,1)S(1)}, bf16[512,512]{1,0:T(8,128)(2,1)}, u32[]{:S(2)}) copy-start(bf16[512,512]{1,0:T(8,128)(2,1)} %add_convert_fusion.1) | copy-start | bytes 1572868
Sparse Core Ops, SparseCore 0:
  8.9 25.2 all-gather.27
  36.4 98.6 all-gather.33
  148.4 38.4 all-gather.35
  188.8 49.0 all-gather.37
  242.2 29.3 reduce-scatter.3
  273.7 22.5 all-gather.29
  298.5 98.6 all-gather.39
  410.5 38.3 all-gather.41
  451.0 49.0 all-gather.43
  504.5 29.3 reduce-scatter.5
  535.9 22.5 all-gather.31
  560.6 98.6 all-gather.45
  672.6 38.4 all-gather.47
  713.0 49.0 all-gather.49
  766.4 29.3 reduce-scatter.7
where the time goes:
time: 806 us; the launch traced here: 804 us
  waiting for transfers between devices  618 us (77%)
  matrix products  62 us (8%)
  blocking collectives  53.2 us (7%)
  other arithmetic  41.7 us (5%)
  local copies, waits for them, and re-layouts  14.5 us (2%)
  between operations  13.8 us (2%)
    all_gather x3, waiting for transfers between devices, local(): lax.all_gather(qkv_weight[layer_index], 'seq', axis=0, tiled=True)  296 us
    all_gather x3, waiting for transfers between devices, local(): lax.all_gather(out_weight[layer_index], 'seq', axis=1, tiled=True)  120 us
    reduce_scatter x3, waiting for transfers between devices, local(): lax.psum_scatter(terms.astype(jnp.bfloat16), 'grp', scatter_dimension=1,...  88.4 us
    all_gather x3, waiting for transfers between devices, local(): gathered = lax.all_gather(stream, 'grp', axis=1, tiled=True)  67.3 us
    all_gather x3, blocking collectives, prefix(): lax.all_gather(part.astype(kind), axis)  53.2 us
    all_gather x3, waiting for transfers between devices, prefix(): lax.all_gather(part.astype(kind), axis)  43.3 us
    select_n x48, other arithmetic, step(): return jax.tree.map(lambda a, b: jnp.where(reached, a, b), new, before)  25.5 us
    dot_general x3, matrix products, local(): jnp.dot(normed, lax.all_gather(qkv_weight[layer_index], 'seq', axis=0, ti...  22.3 us
  transfers between devices with their start and end apart: 15, of which 15 were waited for; matrix products, arithmetic and copies ran while one was open for 7% of the time, Pallas kernels for 0%

commit v1 on v0

--- a/solution.py
+++ b/solution.py
@@ -53,7 +53,14 @@
     stream = hidden
     causal_mask = jnp.arange(token_rows)[:, None] >= jnp.arange(token_rows)[None, :]
     for layer_index in range(layer_count):
-        gathered = lax.all_gather(stream, "grp", axis=1, tiled=True)
+        ring = [stream]
+        for hop in range(3):
+            ring.append(lax.ppermute(ring[-1], "grp", [(dev, (dev + 1) % 4) for dev in range(4)]))
+        gathered = jnp.roll(
+            jnp.concatenate(ring[::-1], axis=1),
+            (lax.axis_index("grp") + 1) * ring[0].shape[1],
+            axis=1,
+        )
         wide = gathered.astype(jnp.float32)
         inverse_rms = lax.rsqrt(jnp.mean(wide * wide, axis=-1, keepdims=True) + 1e-05)
         normed = (wide * inverse_rms * norm_gain[layer_index][None, :]).astype(jnp.bfloat16)

time: 806 us -> 742 us (0.921)
  waiting for transfers between devices: 618 us -> 525 us
  other arithmetic: 41.7 us -> 50.6 us
  matrix products: 62 us -> 70.2 us
    all_gather x3, waiting for transfers between devices: 296 us -> 205 us  [local(): lax.all_gather(qkv_weight[layer_index], 'seq', axis=0, tiled=True)]
    ppermute x0 -> x9, waiting for transfers between devices: none -> 76.9 us  [local(): lax.ppermute(ring[-1], 'grp', [(dev, (dev + 1) % 4) for dev in range(4)])]
    all_gather x3 -> x0, waiting for transfers between devices: 67.3 us -> none  [local(): gathered = lax.all_gather(stream, 'grp', axis=1, tiled=True)]
    reduce_sum x3, other arithmetic: 6.67 us -> 17.3 us  [local(): jnp.mean(wide * wide, axis=-1, keepdims=True) + 1e-05]
  transfers between devices with their start and end apart: 15 -> 21, of which waited for: 15 -> 21; matrix products, arithmetic and copies ran while one was open for 7% -> 11% of each run, Pallas kernels for 0% -> 0%
where the time goes in v1:
time: 742 us; the launch traced here: 735 us
  waiting for transfers between devices  525 us (71%)
  matrix products  70.2 us (9%)
  blocking collectives  53.6 us (7%)
  other arithmetic  50.6 us (7%)
  local copies, waits for them, and re-layouts  18.8 us (3%)
  between operations  14.3 us (2%)
    all_gather x3, waiting for transfers between devices, local(): lax.all_gather(qkv_weight[layer_index], 'seq', axis=0, tiled=True)  205 us
    all_gather x3, waiting for transfers between devices, local(): lax.all_gather(out_weight[layer_index], 'seq', axis=1, tiled=True)  118 us
    reduce_scatter x3, waiting for transfers between devices, local(): lax.psum_scatter(terms.astype(jnp.bfloat16), 'grp', scatter_dimension=1,...  86.9 us
    ppermute x9, waiting for transfers between devices, local(): lax.ppermute(ring[-1], 'grp', [(dev, (dev + 1) % 4) for dev in range(4)])  76.9 us
    all_gather x3, blocking collectives, prefix(): lax.all_gather(part.astype(kind), axis)  53.6 us
    all_gather x3, waiting for transfers between devices, prefix(): lax.all_gather(part.astype(kind), axis)  36.5 us
    select_n x48, other arithmetic, step(): return jax.tree.map(lambda a, b: jnp.where(reached, a, b), new, before)  25.4 us
    dot_general x3, matrix products, local(): jnp.dot(normed, lax.all_gather(qkv_weight[layer_index], 'seq', axis=0, ti...  22.3 us
  transfers between devices with their start and end apart: 21, of which 21 were waited for; matrix products, arithmetic and copies ran while one was open for 11% of the time, Pallas kernels for 0%

profile of v1, /device:TPU:0, one launch (start us, length us, event | category | flops | bytes accessed | tf_op | source)
XLA Modules:
  0.0 735.1 jit_solution(9751079724951482856)
XLA Ops:
  6.5 3.1 fusion.156
  10.3 8.8 %collective-permute-done = bf16[512,512]{1,0:T(8,128)(2,1)S(1)} collective-permute-done((bf16[512,512]{1,0:T(8,128)(2,1)S(1)}, bf16[512,512]{1,0:T(8,128)(2,1)S(1)}, u32[]{:S(2)}, u32[]{:S(2)}) %collective-permute-start) | collective-permute-done | bytes 524320 | tf_op jit(solution)/shard_map/ppermute | solution.py:58
  19.1 8.6 %collective-permute-done.1 = bf16[512,512]{1,0:T(8,128)(2,1)S(1)} collective-permute-done((bf16[512,512]{1,0:T(8,128)(2,1)S(1)}, bf16[512,512]{1,0:T(8,128)(2,1)S(1)}, u32[]{:S(2)}, u32[]{:S(2)}) %collective-permute-start.1) | collective-permute-done | bytes 524320 | tf_op jit(solution)/shard_map/ppermute | solution.py:58
  28.5 7.9 %collective-permute-done.2 = bf16[512,512]{1,0:T(8,128)(2,1)} collective-permute-done((bf16[512,512]{1,0:T(8,128)(2,1)S(1)}, bf16[512,512]{1,0:T(8,128)(2,1)}, u32[]{:S(2)}, u32[]{:S(2)}) %collective-permute-start.2) | collective-permute-done | bytes 524320 | tf_op jit(solution)/shard_map/ppermute | solution.py:58
  36.4 5.9 fusion.6
  42.3 68.9 %all-gather.25.cloned.1.call-done = bf16[1,2048,1536]{2,1,0:T(8,128)(2,1)} async-done(((bf16[1,256,1536]{2,1,0:T(8,128)(2,1)}), bf16[1,2048,1536]{2,1,0:T(8,128)(2,1)}) %all-gather.25.cloned.1.call-update) | async-done | bytes 6291472 | tf_op jit(solution)/shard_map/all_gather | solution.py:69
  111.3 7.4 %fusion.15 = bf16[512,1536]{1,0:T(8,128)(2,1)} fusion(bf16[1,2048,1536]{2,1,0:T(8,128)(2,1)} %all-gather.25.cloned.1.call-done, bf16[512,2048]{1,0:T(8,128)(2,1)S(1)} %get-tuple-element.446, f32[2048]{0:T(1024)S(1)} %bitcast.326, f32[512]{0:T(512)S(1)} %add_rsqrt_fusion.2), kind=kOutput, calls=%fused_computation.57 | convolution fusion | flops 3226206208 | bytes 9971712 | tf_op jit(solution)/shard_map/dot_general | solution.py:67
  121.2 2.3 fusion.163
  127.4 18.0 %all-gather.12 = bf16[8,4,128]{2,1,0:T(4,128)(2,1)S(1)} all-gather(bf16[1,4,128]{2,1,0:T(4,128)(2,1)S(1)} %bitcast.327), channel_id=4, replica_groups=mesh['seq'=8,'grp'=4] {'seq'}, dimensions={0}, use_global_device_ids=true | all-gather | bytes 9216 | tf_op jit(solution)/shard_map/all_gather | solution.py:14
  146.1 2.2 fusion.98
  148.3 3.1 select_reduce_fusion.2
  151.4 11.7 %all-gather.27.cloned.1.call-done = bf16[32,128,128]{2,1,0:T(8,128)(2,1)} async-done(((bf16[4,128,128]{2,1,0:T(8,128)(2,1)}), bf16[32,128,128]{2,1,0:T(8,128)(2,1)}) %all-gather.27.cloned.1.call-update) | async-done | bytes 1048592 | tf_op jit(solution)/shard_map/all_gather | solution.py:14
  163.1 8.6 %while.48 = (s32[]{:T(128)}, f32[4,128,128]{2,1,0:T(8,128)S(1)}, f32[4,128]{1,0:T(4,128)S(1)}, s32[]{:T(128)}, bf16[8,4,128,128]{3,2,1,0:T(8,128)(2,1)}, /*index...) while((s32[]{:T(128)}, f32[4,128,128]{2,1,0:T(8,128)S(1)}, f32[4,128]{1,0:T(4,128)S(1)}, ...), condition=%wide.region_5.7_spmd.clone, body=%wide.region_4.6_spmd.clone.sunk | while | flops 264196 | bytes 660595 | solution.py:31
  172.6 2.2 multiply_reduce_fusion.2
  175.0 39.2 %all-gather.29.cloned.1.call-done = bf16[1,512,2048]{2,1,0:T(8,128)(2,1)} async-done(((bf16[1,512,256]{2,1,0:T(8,128)(2,1)}), bf16[1,512,2048]{2,1,0:T(8,128)(2,1)}) %all-gather.29.cloned.1.call-update) | async-done | bytes 2097168 | tf_op jit(solution)/shard_map/all_gather | solution.py:108
  214.2 4.3 convolution_convert_fusion.2
  219.1 28.9 %reduce-scatter.4.cloned.1.call-done = bf16[512,512]{1,0:T(8,128)(2,1)} async-done(((bf16[512,2048]{1,0:T(8,128)(2,1)}), bf16[512,512]{1,0:T(8,128)(2,1)}) %reduce-scatter.4.cloned.1.call-update) | async-done | bytes 524304 | tf_op jit(solution)/shard_map/reduce_scatter | solution.py:111
  249.2 8.6 %collective-permute-done.3 = bf16[512,512]{1,0:T(8,128)(2,1)S(1)} collective-permute-done((bf16[512,512]{1,0:T(8,128)(2,1)S(1)}, bf16[512,512]{1,0:T(8,128)(2,1)S(1)}, u32[]{:S(2)}, u32[]{:S(2)}) %collective-permute-start.3) | collective-permute-done | bytes 524320 | tf_op jit(solution)/shard_map/ppermute | solution.py:58
  257.8 8.6 %collective-permute-done.4 = bf16[512,512]{1,0:T(8,128)(2,1)S(1)} collective-permute-done((bf16[512,512]{1,0:T(8,128)(2,1)S(1)}, bf16[512,512]{1,0:T(8,128)(2,1)S(1)}, u32[]{:S(2)}, u32[]{:S(2)}) %collective-permute-start.4) | collective-permute-done | bytes 524320 | tf_op jit(solution)/shard_map/ppermute | solution.py:58
  266.9 8.6 %collective-permute-done.5 = bf16[512,512]{1,0:T(8,128)(2,1)S(1)} collective-permute-done((bf16[512,512]{1,0:T(8,128)(2,1)S(1)}, bf16[512,512]{1,0:T(8,128)(2,1)S(1)}, u32[]{:S(2)}, u32[]{:S(2)}) %collective-permute-start.5) | collective-permute-done | bytes 524320 | tf_op jit(solution)/shard_map/ppermute | solution.py:58
  275.5 5.7 fusion.9
  281.3 67.5 %all-gather.31.cloned.1.call-done = bf16[1,2048,1536]{2,1,0:T(8,128)(2,1)} async-done(((bf16[1,256,1536]{2,1,0:T(8,128)(2,1)}), bf16[1,2048,1536]{2,1,0:T(8,128)(2,1)}) %all-gather.31.cloned.1.call-update) | async-done | bytes 6291472 | tf_op jit(solution)/shard_map/all_gather | solution.py:69
  348.8 7.4 %fusion.18 = bf16[512,1536]{1,0:T(8,128)(2,1)} fusion(bf16[1,2048,1536]{2,1,0:T(8,128)(2,1)} %all-gather.31.cloned.1.call-done, bf16[512,2048]{1,0:T(8,128)(2,1)S(1)} %get-tuple-element.444, f32[2048]{0:T(1024)S(1)} %bitcast.325, f32[512]{0:T(512)S(1)} %add_rsqrt_fusion.1), kind=kOutput, calls=%fused_computation.58 | convolution fusion | flops 3226206208 | bytes 9971712 | tf_op jit(solution)/shard_map/dot_general | solution.py:67
  359.4 2.3 fusion.164
  364.4 17.7 %all-gather.13 = bf16[8,4,128]{2,1,0:T(4,128)(2,1)S(1)} all-gather(bf16[1,4,128]{2,1,0:T(4,128)(2,1)S(1)} %bitcast.329), channel_id=8, replica_groups=mesh['seq'=8,'grp'=4] {'seq'}, dimensions={0}, use_global_device_ids=true | all-gather | bytes 9216 | tf_op jit(solution)/shard_map/all_gather | solution.py:14
  383.8 2.2 fusion.96
  386.0 3.4 select_reduce_fusion.1
  389.4 12.7 %all-gather.33.cloned.1.call-done = bf16[32,128,128]{2,1,0:T(8,128)(2,1)} async-done(((bf16[4,128,128]{2,1,0:T(8,128)(2,1)}), bf16[32,128,128]{2,1,0:T(8,128)(2,1)}) %all-gather.33.cloned.1.call-update) | async-done | bytes 1048592 | tf_op jit(solution)/shard_map/all_gather | solution.py:14
  402.1 8.6 %while.49 = (s32[]{:T(128)}, f32[4,128,128]{2,1,0:T(8,128)S(1)}, f32[4,128]{1,0:T(4,128)S(1)}, s32[]{:T(128)}, bf16[8,4,128,128]{3,2,1,0:T(8,128)(2,1)}, /*index...) while((s32[]{:T(128)}, f32[4,128,128]{2,1,0:T(8,128)S(1)}, f32[4,128]{1,0:T(4,128)S(1)}, ...), condition=%wide.region_14.16_spmd.clone, body=%wide.region_13.15_spmd.clone.sunk | while | flops 264196 | bytes 660595 | solution.py:31
  411.6 2.2 multiply_reduce_fusion.1
  414.0 39.2 %all-gather.35.cloned.1.call-done = bf16[1,512,2048]{2,1,0:T(8,128)(2,1)} async-done(((bf16[1,512,256]{2,1,0:T(8,128)(2,1)}), bf16[1,512,2048]{2,1,0:T(8,128)(2,1)}) %all-gather.35.cloned.1.call-update) | async-done | bytes 2097168 | tf_op jit(solution)/shard_map/all_gather | solution.py:108
  453.2 4.2 convolution_convert_fusion.1
  458.4 28.5 %reduce-scatter.6.cloned.1.call-done = bf16[512,512]{1,0:T(8,128)(2,1)} async-done(((bf16[512,2048]{1,0:T(8,128)(2,1)}), bf16[512,512]{1,0:T(8,128)(2,1)}) %reduce-scatter.6.cloned.1.call-update) | async-done | bytes 524304 | tf_op jit(solution)/shard_map/reduce_scatter | solution.py:111
  488.2 8.6 %collective-permute-done.6 = bf16[512,512]{1,0:T(8,128)(2,1)S(1)} collective-permute-done((bf16[512,512]{1,0:T(8,128)(2,1)S(1)}, bf16[512,512]{1,0:T(8,128)(2,1)S(1)}, u32[]{:S(2)}, u32[]{:S(2)}) %collective-permute-start.6) | collective-permute-done | bytes 524320 | tf_op jit(solution)/shard_map/ppermute | solution.py:58
  496.8 8.6 %collective-permute-done.7 = bf16[512,512]{1,0:T(8,128)(2,1)S(1)} collective-permute-done((bf16[512,512]{1,0:T(8,128)(2,1)S(1)}, bf16[512,512]{1,0:T(8,128)(2,1)S(1)}, u32[]{:S(2)}, u32[]{:S(2)}) %collective-permute-start.7) | collective-permute-done | bytes 524320 | tf_op jit(solution)/shard_map/ppermute | solution.py:58
  505.4 8.6 %collective-permute-done.8 = bf16[512,512]{1,0:T(8,128)(2,1)S(1)} collective-permute-done((bf16[512,512]{1,0:T(8,128)(2,1)S(1)}, bf16[512,512]{1,0:T(8,128)(2,1)S(1)}, u32[]{:S(2)}, u32[]{:S(2)}) %collective-permute-start.8) | collective-permute-done | bytes 524320 | tf_op jit(solution)/shard_map/ppermute | solution.py:58
  514.0 5.7 fusion.12
  519.7 68.1 %all-gather.37.cloned.1.call-done = bf16[1,2048,1536]{2,1,0:T(8,128)(2,1)} async-done(((bf16[1,256,1536]{2,1,0:T(8,128)(2,1)}), bf16[1,2048,1536]{2,1,0:T(8,128)(2,1)}) %all-gather.37.cloned.1.call-update) | async-done | bytes 6291472 | tf_op jit(solution)/shard_map/all_gather | solution.py:69
  587.9 7.4 %fusion.21 = bf16[512,1536]{1,0:T(8,128)(2,1)} fusion(bf16[1,2048,1536]{2,1,0:T(8,128)(2,1)} %all-gather.37.cloned.1.call-done, bf16[512,2048]{1,0:T(8,128)(2,1)S(1)} %get-tuple-element.442, f32[2048]{0:T(1024)S(1)} %bitcast.324, f32[512]{0:T(512)S(1)} %add_rsqrt_fusion), kind=kOutput, calls=%fused_computation.59 | convolution fusion | flops 3226206208 | bytes 9971712 | tf_op jit(solution)/shard_map/dot_general | solution.py:67
  598.5 2.3 fusion.165
  603.5 17.9 %all-gather.14 = bf16[8,4,128]{2,1,0:T(4,128)(2,1)S(1)} all-gather(bf16[1,4,128]{2,1,0:T(4,128)(2,1)S(1)} %bitcast.328), channel_id=12, replica_groups=mesh['seq'=8,'grp'=4] {'seq'}, dimensions={0}, use_global_device_ids=true | all-gather | bytes 9216 | tf_op jit(solution)/shard_map/all_gather | solution.py:14
  623.5 2.4 fusion.94
  625.9 3.2 select_reduce_fusion
  629.1 12.1 %all-gather.39.cloned.1.call-done = bf16[32,128,128]{2,1,0:T(8,128)(2,1)} async-done(((bf16[4,128,128]{2,1,0:T(8,128)(2,1)}), bf16[32,128,128]{2,1,0:T(8,128)(2,1)}) %all-gather.39.cloned.1.call-update) | async-done | bytes 1048592 | tf_op jit(solution)/shard_map/all_gather | solution.py:14
  641.2 8.6 %while.50 = (s32[]{:T(128)}, f32[4,128,128]{2,1,0:T(8,128)S(1)}, f32[4,128]{1,0:T(4,128)S(1)}, s32[]{:T(128)}, bf16[8,4,128,128]{3,2,1,0:T(8,128)(2,1)}, /*index...) while((s32[]{:T(128)}, f32[4,128,128]{2,1,0:T(8,128)S(1)}, f32[4,128]{1,0:T(4,128)S(1)}, ...), condition=%wide.region_23.25_spmd.clone, body=%wide.region_22.24_spmd.clone.sunk | while | flops 264196 | bytes 660595 | solution.py:31
  653.1 39.3 %all-gather.41.cloned.1.call-done = bf16[1,512,2048]{2,1,0:T(8,128)(2,1)} async-done(((bf16[1,512,256]{2,1,0:T(8,128)(2,1)}), bf16[1,512,2048]{2,1,0:T(8,128)(2,1)}) %all-gather.41.cloned.1.call-update) | async-done | bytes 2097168 | tf_op jit(solution)/shard_map/all_gather | solution.py:108
  692.3 4.2 convolution_convert_fusion
  696.6 29.5 %reduce-scatter.8.cloned.1.call-done = bf16[512,512]{1,0:T(8,128)(2,1)} async-done(((bf16[512,2048]{1,0:T(8,128)(2,1)}), bf16[512,512]{1,0:T(8,128)(2,1)}) %reduce-scatter.8.cloned.1.call-update) | async-done | bytes 524304 | tf_op jit(solution)/shard_map/reduce_scatter | solution.py:111
  (160 shorter events, 61.2 us)
Async XLA Ops:
  6.5 3.2 copy-start.1
  6.5 21.2 %copy-start.8 = (f32[3,2048]{1,0:T(4,128)S(1)}, f32[3,2048]{1,0:T(4,128)}, u32[]{:S(2)}) copy-start(f32[3,2048]{1,0:T(4,128)} %param.18) | copy-start | bytes 73732
  6.5 104.7 %all-gather.25.cloned.1.call-start = ((), (), s32[]{:S(2)}) async-start(), calls=%async_computation.6 | async-start | bytes 7077888 | tf_op jit(solution)/shard_map/all_gather | solution.py:69
  9.7 153.3 %all-gather.27.cloned.1.call-start = ((), (), s32[]{:S(2)}) async-start(), calls=%async_computation.7 | async-start | bytes 1179648 | tf_op jit(solution)/shard_map/all_gather | solution.py:14
  9.8 9.3 %collective-permute-start = (bf16[512,512]{1,0:T(8,128)(2,1)S(1)}, bf16[512,512]{1,0:T(8,128)(2,1)S(1)}, u32[]{:S(2)}, u32[]{:S(2)}) collective-permute-start(bf16[512,512]{1,0:T(8,128)(2,1)S(1)} %copy-done.1), channel_id=1, source_target_pairs={{0,1},{1,2},{2,3},{3,0},{4,5},{5,6},{6,7},{7,4},{8,9},{9,10},{10,1... | collective-permute-start | bytes 1572872 | tf_op jit(solution)/shard_map/ppermute | solution.py:58
  19.1 8.6 %collective-permute-start.1 = (bf16[512,512]{1,0:T(8,128)(2,1)S(1)}, bf16[512,512]{1,0:T(8,128)(2,1)S(1)}, u32[]{:S(2)}, u32[]{:S(2)}) collective-permute-start(bf16[512,512]{1,0:T(8,128)(2,1)S(1)} %collective-permute-done), channel_id=1, source_target_pairs={{0,1},{1,2},{2,3},{3,0},{4,5},{5,6},{6,7},{7,4},{8,9},{9,10},{10,1... | collective-permute-start | bytes 1572872 | tf_op jit(solution)/shard_map/ppermute | solution.py:58
  27.7 0.8 copy-start.5
  27.7 8.7 %collective-permute-start.2 = (bf16[512,512]{1,0:T(8,128)(2,1)S(1)}, bf16[512,512]{1,0:T(8,128)(2,1)}, u32[]{:S(2)}, u32[]{:S(2)}) collective-permute-start(bf16[512,512]{1,0:T(8,128)(2,1)S(1)} %collective-permute-done.1), channel_id=1, source_target_pairs={{0,1},{1,2},{2,3},{3,0},{4,5},{5,6},{6,7},{7,4},{8,9},{9,10},{10,1... | collective-permute-start | bytes 1572872 | tf_op jit(solution)/shard_map/ppermute | solution.py:58
  120.4 7.0 copy-start.9
  124.4 89.8 %all-gather.29.cloned.1.call-start = ((), (), s32[]{:S(2)}) async-start(), calls=%async_computation.8 | async-start | bytes 2359296 | tf_op jit(solution)/shard_map/all_gather | solution.py:108
  126.5 121.4 %reduce-scatter.4.cloned.1.call-start = ((), (), s32[]{:S(2)}) async-start(), calls=%async_computation.3 | async-start | bytes 2621440 | tf_op jit(solution)/shard_map/reduce_scatter | solution.py:111
  148.3 24.3 %copy-start.6 = (pred[512,512]{0,1:T(8,128)(4,1)S(1)}, pred[512,512]{0,1:T(8,128)(4,1)}, u32[]{:S(2)}) copy-start(pred[512,512]{0,1:T(8,128)(4,1)} %iota_compare_fusion) | copy-start | bytes 786436
  214.2 33.8 %copy-start.2 = (bf16[512,512]{1,0:T(8,128)(2,1)S(1)}, bf16[512,512]{1,0:T(8,128)(2,1)}, u32[]{:S(2)}) copy-start(bf16[512,512]{1,0:T(8,128)(2,1)} %param.14) | copy-start | bytes 1572868
  218.5 130.3 %all-gather.31.cloned.1.call-start = ((), (), s32[]{:S(2)}) async-start(), calls=%async_computation.9 | async-start | bytes 7077888 | tf_op jit(solution)/shard_map/all_gather | solution.py:69
  219.1 183.0 %all-gather.33.cloned.1.call-start = ((), (), s32[]{:S(2)}) async-start(), calls=%async_computation.10 | async-start | bytes 1179648 | tf_op jit(solution)/shard_map/all_gather | solution.py:14
  249.2 8.7 %collective-permute-start.3 = (bf16[512,512]{1,0:T(8,128)(2,1)S(1)}, bf16[512,512]{1,0:T(8,128)(2,1)S(1)}, u32[]{:S(2)}, u32[]{:S(2)}) collective-permute-start(bf16[512,512]{1,0:T(8,128)(2,1)S(1)} %add_convert_fusion.2), channel_id=1, source_target_pairs={{0,1},{1,2},{2,3},{3,0},{4,5},{5,6},{6,7},{7,4},{8,9},{9,10},{10,1... | collective-permute-start | bytes 1572872 | tf_op jit(solution)/shard_map/ppermute | solution.py:58
  257.8 8.6 %collective-permute-start.4 = (bf16[512,512]{1,0:T(8,128)(2,1)S(1)}, bf16[512,512]{1,0:T(8,128)(2,1)S(1)}, u32[]{:S(2)}, u32[]{:S(2)}) collective-permute-start(bf16[512,512]{1,0:T(8,128)(2,1)S(1)} %collective-permute-done.3), channel_id=1, source_target_pairs={{0,1},{1,2},{2,3},{3,0},{4,5},{5,6},{6,7},{7,4},{8,9},{9,10},{10,1... | collective-permute-start | bytes 1572872 | tf_op jit(solution)/shard_map/ppermute | solution.py:58
  266.4 9.1 %collective-permute-start.5 = (bf16[512,512]{1,0:T(8,128)(2,1)S(1)}, bf16[512,512]{1,0:T(8,128)(2,1)S(1)}, u32[]{:S(2)}, u32[]{:S(2)}) collective-permute-start(bf16[512,512]{1,0:T(8,128)(2,1)S(1)} %collective-permute-done.4), channel_id=1, source_target_pairs={{0,1},{1,2},{2,3},{3,0},{4,5},{5,6},{6,7},{7,4},{8,9},{9,10},{10,1... | collective-permute-start | bytes 1572872 | tf_op jit(solution)/shard_map/ppermute | solution.py:58
  361.7 0.8 copy-start.4
  363.6 89.7 %all-gather.35.cloned.1.call-start = ((), (), s32[]{:S(2)}) async-start(), calls=%async_computation.11 | async-start | bytes 2359296 | tf_op jit(solution)/shard_map/all_gather | solution.py:108
  364.3 122.6 %reduce-scatter.6.cloned.1.call-start = ((), (), s32[]{:S(2)}) async-start(), calls=%async_computation.4 | async-start | bytes 2621440 | tf_op jit(solution)/shard_map/reduce_scatter | solution.py:111
  386.0 25.7 %copy-start.7 = (pred[512,512]{0,1:T(8,128)(4,1)S(1)}, pred[512,512]{0,1:T(8,128)(4,1)}, u32[]{:S(2)}) copy-start(pred[512,512]{0,1:T(8,128)(4,1)} %iota_compare_fusion) | copy-start | bytes 786436
  457.5 130.4 %all-gather.37.cloned.1.call-start = ((), (), s32[]{:S(2)}) async-start(), calls=%async_computation.12 | async-start | bytes 7077888 | tf_op jit(solution)/shard_map/all_gather | solution.py:69
  458.2 183.0 %all-gather.39.cloned.1.call-start = ((), (), s32[]{:S(2)}) async-start(), calls=%async_computation.13 | async-start | bytes 1179648 | tf_op jit(solution)/shard_map/all_gather | solution.py:14
  488.1 8.7 %collective-permute-start.6 = (bf16[512,512]{1,0:T(8,128)(2,1)S(1)}, bf16[512,512]{1,0:T(8,128)(2,1)S(1)}, u32[]{:S(2)}, u32[]{:S(2)}) collective-permute-start(bf16[512,512]{1,0:T(8,128)(2,1)S(1)} %add_convert_fusion.1), channel_id=1, source_target_pairs={{0,1},{1,2},{2,3},{3,0},{4,5},{5,6},{6,7},{7,4},{8,9},{9,10},{10,1... | collective-permute-start | bytes 1572872 | tf_op jit(solution)/shard_map/ppermute | solution.py:58
  496.8 8.6 %collective-permute-start.7 = (bf16[512,512]{1,0:T(8,128)(2,1)S(1)}, bf16[512,512]{1,0:T(8,128)(2,1)S(1)}, u32[]{:S(2)}, u32[]{:S(2)}) collective-permute-start(bf16[512,512]{1,0:T(8,128)(2,1)S(1)} %collective-permute-done.6), channel_id=1, source_target_pairs={{0,1},{1,2},{2,3},{3,0},{4,5},{5,6},{6,7},{7,4},{8,9},{9,10},{10,1... | collective-permute-start | bytes 1572872 | tf_op jit(solution)/shard_map/ppermute | solution.py:58
  505.4 8.6 %collective-permute-start.8 = (bf16[512,512]{1,0:T(8,128)(2,1)S(1)}, bf16[512,512]{1,0:T(8,128)(2,1)S(1)}, u32[]{:S(2)}, u32[]{:S(2)}) collective-permute-start(bf16[512,512]{1,0:T(8,128)(2,1)S(1)} %collective-permute-done.7), channel_id=1, source_target_pairs={{0,1},{1,2},{2,3},{3,0},{4,5},{5,6},{6,7},{7,4},{8,9},{9,10},{10,1... | collective-permute-start | bytes 1572872 | tf_op jit(solution)/shard_map/ppermute | solution.py:58
  600.8 0.8 copy-start.3
  602.7 89.7 %all-gather.41.cloned.1.call-start = ((), (), s32[]{:S(2)}) async-start(), calls=%async_computation.14 | async-start | bytes 2359296 | tf_op jit(solution)/shard_map/all_gather | solution.py:108
  603.4 122.7 %reduce-scatter.8.cloned.1.call-start = ((), (), s32[]{:S(2)}) async-start(), calls=%async_computation.5 | async-start | bytes 2621440 | tf_op jit(solution)/shard_map/reduce_scatter | solution.py:111
  622.7 0.8 copy-start
Sparse Core Ops, SparseCore 0:
  9.8 101.4 all-gather.24
  124.6 38.4 all-gather.26
  165.1 49.0 all-gather.28
  218.6 29.3 reduce-scatter.3
  250.0 98.6 all-gather.30
  363.7 38.3 all-gather.32
  404.1 49.0 all-gather.34
  457.6 29.3 reduce-scatter.5
  489.1 98.6 all-gather.36
  602.8 38.3 all-gather.38
  643.3 49.0 all-gather.40
  696.7 29.3 reduce-scatter.7
